TPU v7x, 32 devices: a whole 2x2x4 slice. The times are simulated.
32 devices in a mesh: img: 8 (over z, core), txt: 4 (over y, x).
Axes of the slice: x: 2, y: 2, z: 4, core: 2. Of those that a mesh axis runs over, the one named last changes fastest.
Arguments:
- teacher_img: bfloat16 [8192, 1280], P('img'), may hold values from -40 to 40
- teacher_txt: bfloat16 [4096, 1280], P('txt'), may hold values from -40 to 40
- student_img: bfloat16 [8192, 512], P('img'), may hold values from -40 to 40
- student_txt: bfloat16 [4096, 512], P('txt'), may hold values from -40 to 40
Outputs:
- loss: float32 [], replicated
- grad_img: float32 [8192, 512], P(('img', 'txt'))
- grad_txt: float32 [4096, 512], P(('txt', 'img'))
All inputs are finite; a program needn't handle non-finite values.
Results may differ from a plain program's by a relative error of at most 0.0033.
Values sent between devices are 32-bit elements; how exact they have to be, the bound alone decides.
A program may use at most 64 MiB of HBM per device.

v0:
```python
import math
import jax
import jax.numpy as jnp
from jax import lax
from jax.sharding import PartitionSpec as P


def body(teacher_img, teacher_txt, student_img, student_txt):
    scale_teach = 3.0 / math.sqrt(teacher_img.shape[1])
    scale_learn = 3.0 / math.sqrt(student_img.shape[1])
    rows = teacher_img.shape[0]
    cols = teacher_txt.shape[0]
    img_count = lax.axis_size("img")
    txt_count = lax.axis_size("txt")
    teacher = scale_teach * jnp.einsum(
        "id,jd->ij", teacher_img, teacher_txt, preferred_element_type=jnp.float32
    )
    student = scale_learn * jnp.einsum(
        "id,jd->ij", student_img, student_txt, preferred_element_type=jnp.float32
    )
    row_tpeak, row_lpeak = lax.pmax((jnp.max(teacher, axis=1), jnp.max(student, axis=1)), "txt")
    col_tpeak, col_lpeak = lax.pmax((jnp.max(teacher, axis=0), jnp.max(student, axis=0)), "img")
    row_tmass, row_lmass = lax.psum(
        (
            jnp.sum(jnp.exp(teacher - row_tpeak[:, None]), axis=1),
            jnp.sum(jnp.exp(student - row_lpeak[:, None]), axis=1),
        ),
        "txt",
    )
    col_tmass, col_lmass = lax.psum(
        (
            jnp.sum(jnp.exp(teacher - col_tpeak[None, :]), axis=0),
            jnp.sum(jnp.exp(student - col_lpeak[None, :]), axis=0),
        ),
        "img",
    )
    row_teach = row_tpeak + jnp.log(row_tmass)
    row_learn = row_lpeak + jnp.log(row_lmass)
    col_teach = col_tpeak + jnp.log(col_tmass)
    col_learn = col_lpeak + jnp.log(col_lmass)
    p_row = jnp.exp(teacher - row_teach[:, None])
    q_row = jnp.exp(student - row_learn[:, None])
    p_col = jnp.exp(teacher - col_teach[None, :])
    q_col = jnp.exp(student - col_learn[None, :])
    gap = teacher - student
    row_part = (jnp.sum(p_row * gap) + jnp.sum(row_learn - row_teach) / txt_count) / (
        rows * img_count
    )
    col_part = (jnp.sum(p_col * gap) + jnp.sum(col_learn - col_teach) / img_count) / (
        cols * txt_count
    )
    delta = (8.0 * (q_row - p_row + q_col - p_col)).astype(jnp.bfloat16)
    loss = 0.5 * lax.psum(row_part + col_part, ("img", "txt"))
    picked = delta
    grad_txt = lax.psum_scatter(
        scale_learn
        * jnp.einsum("ij,id->jd", picked, student_img, preferred_element_type=jnp.float32),
        "img",
        scatter_dimension=0,
        tiled=True,
    )
    picked = delta
    grad_img = lax.psum_scatter(
        scale_learn * jnp.dot(picked, student_txt, preferred_element_type=jnp.float32),
        "txt",
        scatter_dimension=0,
        tiled=True,
    )
    return (loss, grad_img, grad_txt)


def solution(mesh):
    placed = (P("img", None), P("txt", None), P("img", None), P("txt", None))
    return jax.shard_map(
        body,
        mesh=mesh,
        in_specs=placed,
        out_specs=(P(), P(("img", "txt"), None), P(("txt", "img"), None)),
        check_vma=False,
    )
```

profile of v0, /device:TPU:0, one launch (start us, length us, event | category | flops | bytes accessed | tf_op | source)
XLA Modules:
  0.0 193.4 jit_solution(10971360036748988000)
XLA Ops:
  7.2 0.0 copy-start
  7.2 0.0 reduce-scatter.3.cloned.1.call-start
  7.2 1.7 copy-done
  8.9 0.0 copy-start.2
  8.9 0.0 copy-start.4
  8.9 6.4 %multiply_reduce_fusion.4 = (f32[1024]{0:T(1024)S(1)}, f32[1024]{0:T(1024)S(1)}, f32[1024,1024]{1,0:T(8,128)}) fusion(bf16[1024,1280]{1,0:T(8,128)(2,1)S(1)} %copy-done, bf16[1024,1280]{1,0:T(8,128)(2,1)} %param.5), kind=kOutput, calls=%fused_computation.12 | convolution fusion | flops 2687498240 | bytes 9445376 | tf_op jit(solution)/shard_map/id,jd->ij/dot_general | solution.py:15
  15.3 0.0 copy-done.2
  15.3 0.0 copy-done.4
  15.3 3.2 %multiply_reduce_fusion.2 = (f32[1024]{0:T(1024)S(1)}, f32[1024]{0:T(1024)S(1)}, f32[1024,1024]{1,0:T(8,128)}) fusion(bf16[1024,512]{1,0:T(8,128)(2,1)S(1)} %copy-done.4, bf16[1024,512]{1,0:T(8,128)(2,1)S(1)} %copy-done.2), kind=kOutput, calls=%fused_computation.9 | convolution fusion | flops 1076885504 | bytes 6299648 | tf_op jit(solution)/shard_map/id,jd->ij/dot_general | solution.py:18
  18.5 18.3 %all-reduce = (f32[1024]{0:T(1024)S(1)}, f32[1024]{0:T(1024)S(1)}) all-reduce(f32[1024]{0:T(1024)S(1)} %get-tuple-element.11, f32[1024]{0:T(1024)S(1)} %get-tuple-element.6), channel_id=1, replica_groups=mesh['img'=8,'txt'=4] {'img'}, use_global_device_ids=true, to_apply=%region_11.0 | all-reduce | flops 2048 | bytes 16384 | tf_op jit(solution)/shard_map/pmax | solution.py:22
  36.9 10.1 %all-reduce.1 = (f32[1024]{0:T(1024)S(1)}, f32[1024]{0:T(1024)S(1)}) all-reduce(f32[1024]{0:T(1024)S(1)} %get-tuple-element.12, f32[1024]{0:T(1024)S(1)} %get-tuple-element.7), channel_id=1, replica_groups=mesh['img'=8,'txt'=4] {'txt'}, use_global_device_ids=true, to_apply=%region_1.0 | all-reduce | flops 2048 | bytes 16384 | tf_op jit(solution)/shard_map/pmax | solution.py:21
  47.0 3.7 %exponential_reduce_fusion.1 = (f32[1024]{0:T(1024)S(1)}, f32[1024]{0:T(1024)S(1)}) fusion(f32[1024,1024]{1,0:T(8,128)} %get-tuple-element.21, f32[1024]{0:T(1024)S(1)} %get-tuple-element.13, f32[1024]{0:T(1024)S(1)} %get-tuple-element.15), kind=kLoop, calls=%fused_computation.4 | loop fusion | flops 5240832 | bytes 4210688 | tf_op jit(solution)/shard_map/reduce_sum | solution.py:32
  50.7 13.6 %psum.37 = f32[1024]{0:T(1024)S(1)} all-reduce(f32[1024]{0:T(1024)S(1)} %get-tuple-element.9), channel_id=1, replica_groups=mesh['img'=8,'txt'=4] {'img'}, use_global_device_ids=true, to_apply=%region_13.0 | all-reduce | flops 1024 | bytes 8192 | tf_op jit(solution)/shard_map/psum | solution.py:30
  64.3 7.9 %psum.35 = f32[1024]{0:T(1024)S(1)} all-reduce(f32[1024]{0:T(1024)S(1)} %get-tuple-element.10), channel_id=1, replica_groups=mesh['img'=8,'txt'=4] {'txt'}, use_global_device_ids=true, to_apply=%region_3.0 | all-reduce | flops 1024 | bytes 8192 | tf_op jit(solution)/shard_map/psum | solution.py:23
  72.2 8.1 %multiply_reduce_fusion = (f32[]{:T(128)}, f32[]{:T(128)}, f32[1024]{0:T(1024)S(1)}, f32[1024]{0:T(1024)S(1)}) fusion(f32[1024,1024]{1,0:T(8,128)} %get-tuple-element.22, f32[1024,1024]{1,0:T(8,128)} %get-tuple-element.21, f32[1024]{0:T(1024)S(1)} %log_add_fusion.1, f32[1024]{0:T(1024)S(1)} %log_add_fusion.3, f32[1024]{0:T(1024)S(1)} %get-tuple-element.14, ...), kind=kLoop, calls=%fused_computation.2 | loop fusion | flops 13629438 | bytes 8413192 | tf_op jit(solution)/shard_map/reduce_sum | solution.py:49
  80.4 13.6 %psum.38 = f32[1024]{0:T(1024)S(1)} all-reduce(f32[1024]{0:T(1024)S(1)} %get-tuple-element.5), channel_id=1, replica_groups=mesh['img'=8,'txt'=4] {'img'}, use_global_device_ids=true, to_apply=%region_18.0 | all-reduce | flops 1024 | bytes 8192 | tf_op jit(solution)/shard_map/psum | solution.py:30
  93.9 0.6 subtract_reduce_fusion
  94.5 9.0 %psum.36 = f32[1024]{0:T(1024)S(1)} all-reduce(f32[1024]{0:T(1024)S(1)} %get-tuple-element.8), channel_id=1, replica_groups=mesh['img'=8,'txt'=4] {'txt'}, use_global_device_ids=true, to_apply=%region_8.0 | all-reduce | flops 1024 | bytes 8192 | tf_op jit(solution)/shard_map/psum | solution.py:23
  103.5 0.6 subtract_reduce_fusion.1
  104.2 0.0 copy-start.3
  104.2 5.1 %multiply_convert_fusion = bf16[1024,1024]{1,0:T(8,128)(2,1)S(1)} fusion(f32[1024,1024]{1,0:T(8,128)} %get-tuple-element.22, f32[1024,1024]{1,0:T(8,128)} %get-tuple-element.21, f32[1024]{0:T(1024)S(1)} %get-tuple-element.18, f32[1024]{0:T(1024)S(1)} %get-tuple-element.20, f32[1024]{0:T(1024)S(1)} %log_add_fusion.1, f32[1024]{0:T(1024)S(1)} %log_add_fusion.3), kind=kLoop, calls=%fused_computation | loop fusion | flops 11534336 | bytes 10502144 | tf_op jit(solution)/shard_map/convert_element_type | solution.py:52
  109.2 0.0 copy-start.1
  109.2 1.3 copy-done.1
  110.6 0.0 copy-done.3
  110.6 2.6 %convolution_multiply_fusion.1 = f32[1024,512]{1,0:T(8,128)} fusion(bf16[1024,1024]{1,0:T(8,128)(2,1)S(1)} %multiply_convert_fusion, bf16[1024,512]{1,0:T(8,128)(2,1)S(1)} %copy-done.3), kind=kOutput, calls=%fused_computation.15 | convolution fusion | flops 1074266112 | bytes 5242880 | tf_op jit(solution)/shard_map/dot_general | solution.py:64
  113.2 0.0 reduce-scatter.3.cloned.1.call-update
  113.2 0.0 reduce-scatter.5.cloned.1.call-start
  113.2 4.4 %convolution_multiply_fusion = f32[1024,512]{1,0:T(8,128)} fusion(bf16[1024,1024]{1,0:T(8,128)(2,1)} %copy-done.1, bf16[1024,512]{1,0:T(8,128)(2,1)} %param.6), kind=kOutput, calls=%fused_computation.14 | convolution fusion | flops 1074266112 | bytes 5242880 | tf_op jit(solution)/shard_map/ij,id->jd/dot_general | solution.py:57
  117.7 0.0 reduce-scatter.5.cloned.1.call-update
  120.1 37.2 %psum.39 = f32[]{:T(128)} all-reduce(f32[]{:T(128)S(6)} %add.44), channel_id=1, replica_groups=mesh['img'=8,'txt'=4] {'img','txt'}, use_global_device_ids=true, to_apply=%region_20.0 | all-reduce | flops 1 | bytes 8 | tf_op jit(solution)/shard_map/psum | solution.py:53
  158.0 0.0 reduce-scatter.3.cloned.1.call-done
  158.0 27.5 %reduce-scatter.5.cloned.1.call-done = f32[128,512]{1,0:T(8,128)} async-done(((f32[1024,512]{1,0:T(8,128)}), f32[128,512]{1,0:T(8,128)}) %reduce-scatter.5.cloned.1.call-update) | async-done | bytes 262160 | tf_op jit(solution)/shard_map/reduce_scatter | solution.py:55
  (2 shorter events, 0.0 us)
Async XLA Ops:
  7.2 1.7 copy-start
  7.2 150.8 %reduce-scatter.3.cloned.1.call-start = ((), (), s32[]{:S(2)}) async-start(), calls=%async_computation.2 | async-start | bytes 2621440 | tf_op jit(solution)/shard_map/reduce_scatter | solution.py:63
  8.9 6.4 %copy-start.2 = (bf16[1024,512]{1,0:T(8,128)(2,1)S(1)}, bf16[1024,512]{1,0:T(8,128)(2,1)}, u32[]{:S(2)}) copy-start(bf16[1024,512]{1,0:T(8,128)(2,1)} %param.7) | copy-start | bytes 3145732
  8.9 6.4 %copy-start.4 = (bf16[1024,512]{1,0:T(8,128)(2,1)S(1)}, bf16[1024,512]{1,0:T(8,128)(2,1)}, u32[]{:S(2)}) copy-start(bf16[1024,512]{1,0:T(8,128)(2,1)} %param.6) | copy-start | bytes 3145732
  104.2 6.4 %copy-start.3 = (bf16[1024,512]{1,0:T(8,128)(2,1)S(1)}, bf16[1024,512]{1,0:T(8,128)(2,1)}, u32[]{:S(2)}) copy-start(bf16[1024,512]{1,0:T(8,128)(2,1)} %param.7) | copy-start | bytes 3145732
  109.2 1.3 copy-start.1
  113.2 72.3 %reduce-scatter.5.cloned.1.call-start = ((), (), s32[]{:S(2)}) async-start(), calls=%async_computation.3 | async-start | bytes 2359296 | tf_op jit(solution)/shard_map/reduce_scatter | solution.py:55
Sparse Core Ops, SparseCore 0:
  113.3 33.0 reduce-scatter.2
  149.3 36.1 reduce-scatter.4
where the time goes:
time: 194 us; the launch traced here: 193 us
  blocking collectives  110 us (57%)
  waiting for transfers between devices  27.5 us (14%)
  between operations  18.3 us (9%)
  other arithmetic  18.2 us (9%)
  matrix products  16.7 us (9%)
  local copies, waits for them, and re-layouts  3.03 us (2%)
    psum x1, blocking collectives, body(): loss = 0.5 * lax.psum(row_part + col_part, ('img', 'txt'))  37.2 us
    reduce_scatter x1, waiting for transfers between devices, body(): lax.psum_scatter(scale_learn * jnp.einsum('ij,id->jd', picked, student_im...  27.5 us
    psum x2, blocking collectives, body(): lax.psum((jnp.sum(jnp.exp(teacher - col_tpeak[None, :]), axis=0), jnp.sum...  27.2 us
    pmax x1, blocking collectives, body(): lax.pmax((jnp.max(teacher, axis=0), jnp.max(student, axis=0)), 'img')  18.3 us
    psum x2, blocking collectives, body(): lax.psum((jnp.sum(jnp.exp(teacher - row_tpeak[:, None]), axis=1), jnp.sum...  16.9 us
    pmax x1, blocking collectives, body(): lax.pmax((jnp.max(teacher, axis=1), jnp.max(student, axis=1)), 'txt')  10.1 us
    reduce_sum x1, other arithmetic, body(): jnp.sum(p_col * gap) + jnp.sum(col_learn - col_teach) / img_count  8.12 us
    dot_general x1, matrix products, body(): jnp.einsum('id,jd->ij', teacher_img, teacher_txt, preferred_element_type=...  6.41 us
  transfers between devices with their start and end apart: 2, of which 1 were waited for; matrix products, arithmetic and copies ran while one was open for 2% of the time, Pallas kernels for 0%

commit v1 on v0

--- a/solution.py
+++ b/solution.py
@@ -50,7 +50,7 @@
         cols * txt_count
     )
     delta = (8.0 * (q_row - p_row + q_col - p_col)).astype(jnp.bfloat16)
-    loss = 0.5 * lax.psum(row_part + col_part, ("img", "txt"))
+    loss = 0.5 * lax.psum(lax.psum(row_part + col_part, "txt"), "img")
     picked = delta
     grad_txt = lax.psum_scatter(
         scale_learn

time: 194 us -> 193 us (level)
  blocking collectives: 110 us -> 95.7 us
  waiting for transfers between devices: 27.5 us -> 40.7 us
    psum x1 -> x2, blocking collectives: 37.2 us -> 23.2 us  [body(): loss = 0.5 * lax.psum(lax.psum(row_part + col_part, 'txt'), 'img')]
    reduce_scatter x1, waiting for transfers between devices: 27.5 us -> 38.8 us  [body(): lax.psum_scatter(scale_learn * jnp.einsum('ij,id->jd', picked, student_im...]
  transfers between devices with their start and end apart: 2 -> 2, of which waited for: 1 -> 2; matrix products, arithmetic and copies ran while one was open for 2% -> 2% of each run, Pallas kernels for 0% -> 0%
where the time goes in v1:
time: 193 us
  blocking collectives  95.7 us (50%)
  waiting for transfers between devices  40.7 us (21%)
  between operations  18.3 us (9%)
  other arithmetic  18.2 us (9%)
  matrix products  16.7 us (9%)
  local copies, waits for them, and re-layouts  3.03 us (2%)
    reduce_scatter x1, waiting for transfers between devices, body(): lax.psum_scatter(scale_learn * jnp.einsum('ij,id->jd', picked, student_im...  38.8 us
    psum x2, blocking collectives, body(): lax.psum((jnp.sum(jnp.exp(teacher - col_tpeak[None, :]), axis=0), jnp.sum...  27.2 us
    psum x2, blocking collectives, body(): loss = 0.5 * lax.psum(lax.psum(row_part + col_part, 'txt'), 'img')  23.2 us
    pmax x1, blocking collectives, body(): lax.pmax((jnp.max(teacher, axis=0), jnp.max(student, axis=0)), 'img')  18.3 us
    psum x2, blocking collectives, body(): lax.psum((jnp.sum(jnp.exp(teacher - row_tpeak[:, None]), axis=1), jnp.sum...  16.9 us
    pmax x1, blocking collectives, body(): lax.pmax((jnp.max(teacher, axis=1), jnp.max(student, axis=1)), 'txt')  10.1 us
    reduce_sum x1, other arithmetic, body(): jnp.sum(p_col * gap) + jnp.sum(col_learn - col_teach) / img_count  8.12 us
    dot_general x1, matrix products, body(): jnp.einsum('id,jd->ij', teacher_img, teacher_txt, preferred_element_type=...  6.41 us
  transfers between devices with their start and end apart: 2, of which 2 were waited for; matrix products, arithmetic and copies ran while one was open for 2% of the time, Pallas kernels for 0%

profile of v1, /device:TPU:0, one launch (start us, length us, event | category | flops | bytes accessed | tf_op | source)
XLA Modules:
  0.0 192.6 jit_solution(4732662656904826922)
XLA Ops:
  7.2 0.0 copy-start
  7.2 0.0 reduce-scatter.3.cloned.1.call-start
  7.2 1.7 copy-done
  8.9 0.0 copy-start.2
  8.9 0.0 copy-start.4
  8.9 6.4 %multiply_reduce_fusion.4 = (f32[1024]{0:T(1024)S(1)}, f32[1024]{0:T(1024)S(1)}, f32[1024,1024]{1,0:T(8,128)}) fusion(bf16[1024,1280]{1,0:T(8,128)(2,1)S(1)} %copy-done, bf16[1024,1280]{1,0:T(8,128)(2,1)} %param.5), kind=kOutput, calls=%fused_computation.12 | convolution fusion | flops 2687498240 | bytes 9445376 | tf_op jit(solution)/shard_map/id,jd->ij/dot_general | solution.py:15
  15.3 0.0 copy-done.2
  15.3 0.0 copy-done.4
  15.3 3.2 %multiply_reduce_fusion.2 = (f32[1024]{0:T(1024)S(1)}, f32[1024]{0:T(1024)S(1)}, f32[1024,1024]{1,0:T(8,128)}) fusion(bf16[1024,512]{1,0:T(8,128)(2,1)S(1)} %copy-done.4, bf16[1024,512]{1,0:T(8,128)(2,1)S(1)} %copy-done.2), kind=kOutput, calls=%fused_computation.9 | convolution fusion | flops 1076885504 | bytes 6299648 | tf_op jit(solution)/shard_map/id,jd->ij/dot_general | solution.py:18
  18.5 18.3 %all-reduce = (f32[1024]{0:T(1024)S(1)}, f32[1024]{0:T(1024)S(1)}) all-reduce(f32[1024]{0:T(1024)S(1)} %get-tuple-element.11, f32[1024]{0:T(1024)S(1)} %get-tuple-element.6), channel_id=1, replica_groups=mesh['img'=8,'txt'=4] {'img'}, use_global_device_ids=true, to_apply=%region_11.0 | all-reduce | flops 2048 | bytes 16384 | tf_op jit(solution)/shard_map/pmax | solution.py:22
  36.9 10.1 %all-reduce.1 = (f32[1024]{0:T(1024)S(1)}, f32[1024]{0:T(1024)S(1)}) all-reduce(f32[1024]{0:T(1024)S(1)} %get-tuple-element.12, f32[1024]{0:T(1024)S(1)} %get-tuple-element.7), channel_id=1, replica_groups=mesh['img'=8,'txt'=4] {'txt'}, use_global_device_ids=true, to_apply=%region_1.0 | all-reduce | flops 2048 | bytes 16384 | tf_op jit(solution)/shard_map/pmax | solution.py:21
  47.0 3.7 %exponential_reduce_fusion.1 = (f32[1024]{0:T(1024)S(1)}, f32[1024]{0:T(1024)S(1)}) fusion(f32[1024,1024]{1,0:T(8,128)} %get-tuple-element.21, f32[1024]{0:T(1024)S(1)} %get-tuple-element.13, f32[1024]{0:T(1024)S(1)} %get-tuple-element.15), kind=kLoop, calls=%fused_computation.4 | loop fusion | flops 5240832 | bytes 4210688 | tf_op jit(solution)/shard_map/reduce_sum | solution.py:32
  50.7 13.6 %psum.44 = f32[1024]{0:T(1024)S(1)} all-reduce(f32[1024]{0:T(1024)S(1)} %get-tuple-element.9), channel_id=1, replica_groups=mesh['img'=8,'txt'=4] {'img'}, use_global_device_ids=true, to_apply=%region_13.0 | all-reduce | flops 1024 | bytes 8192 | tf_op jit(solution)/shard_map/psum | solution.py:30
  64.3 7.9 %psum.42 = f32[1024]{0:T(1024)S(1)} all-reduce(f32[1024]{0:T(1024)S(1)} %get-tuple-element.10), channel_id=1, replica_groups=mesh['img'=8,'txt'=4] {'txt'}, use_global_device_ids=true, to_apply=%region_3.0 | all-reduce | flops 1024 | bytes 8192 | tf_op jit(solution)/shard_map/psum | solution.py:23
  72.2 8.1 %multiply_reduce_fusion = (f32[]{:T(128)}, f32[]{:T(128)}, f32[1024]{0:T(1024)S(1)}, f32[1024]{0:T(1024)S(1)}) fusion(f32[1024,1024]{1,0:T(8,128)} %get-tuple-element.22, f32[1024,1024]{1,0:T(8,128)} %get-tuple-element.21, f32[1024]{0:T(1024)S(1)} %log_add_fusion.1, f32[1024]{0:T(1024)S(1)} %log_add_fusion.3, f32[1024]{0:T(1024)S(1)} %get-tuple-element.14, ...), kind=kLoop, calls=%fused_computation.2 | loop fusion | flops 13629438 | bytes 8413192 | tf_op jit(solution)/shard_map/reduce_sum | solution.py:49
  80.4 13.6 %psum.45 = f32[1024]{0:T(1024)S(1)} all-reduce(f32[1024]{0:T(1024)S(1)} %get-tuple-element.5), channel_id=1, replica_groups=mesh['img'=8,'txt'=4] {'img'}, use_global_device_ids=true, to_apply=%region_18.0 | all-reduce | flops 1024 | bytes 8192 | tf_op jit(solution)/shard_map/psum | solution.py:30
  93.9 0.6 subtract_reduce_fusion
  94.5 9.0 %psum.43 = f32[1024]{0:T(1024)S(1)} all-reduce(f32[1024]{0:T(1024)S(1)} %get-tuple-element.8), channel_id=1, replica_groups=mesh['img'=8,'txt'=4] {'txt'}, use_global_device_ids=true, to_apply=%region_8.0 | all-reduce | flops 1024 | bytes 8192 | tf_op jit(solution)/shard_map/psum | solution.py:23
  103.5 0.6 subtract_reduce_fusion.1
  104.2 0.0 copy-start.3
  104.2 5.1 %multiply_convert_fusion = bf16[1024,1024]{1,0:T(8,128)(2,1)S(1)} fusion(f32[1024,1024]{1,0:T(8,128)} %get-tuple-element.22, f32[1024,1024]{1,0:T(8,128)} %get-tuple-element.21, f32[1024]{0:T(1024)S(1)} %get-tuple-element.18, f32[1024]{0:T(1024)S(1)} %get-tuple-element.20, f32[1024]{0:T(1024)S(1)} %log_add_fusion.1, f32[1024]{0:T(1024)S(1)} %log_add_fusion.3), kind=kLoop, calls=%fused_computation | loop fusion | flops 11534336 | bytes 10502144 | tf_op jit(solution)/shard_map/convert_element_type | solution.py:52
  109.2 0.0 copy-start.1
  109.2 1.3 copy-done.1
  110.6 0.0 copy-done.3
  110.6 2.6 %convolution_multiply_fusion.1 = f32[1024,512]{1,0:T(8,128)} fusion(bf16[1024,1024]{1,0:T(8,128)(2,1)S(1)} %multiply_convert_fusion, bf16[1024,512]{1,0:T(8,128)(2,1)S(1)} %copy-done.3), kind=kOutput, calls=%fused_computation.15 | convolution fusion | flops 1074266112 | bytes 5242880 | tf_op jit(solution)/shard_map/dot_general | solution.py:64
  113.2 0.0 reduce-scatter.3.cloned.1.call-update
  113.2 0.0 reduce-scatter.5.cloned.1.call-start
  113.2 4.4 %convolution_multiply_fusion = f32[1024,512]{1,0:T(8,128)} fusion(bf16[1024,1024]{1,0:T(8,128)(2,1)} %copy-done.1, bf16[1024,512]{1,0:T(8,128)(2,1)} %param.6), kind=kOutput, calls=%fused_computation.14 | convolution fusion | flops 1074266112 | bytes 5242880 | tf_op jit(solution)/shard_map/ij,id->jd/dot_general | solution.py:57
  117.7 0.0 reduce-scatter.5.cloned.1.call-update
  120.1 9.0 %psum.46 = f32[]{:T(128)} all-reduce(f32[]{:T(128)S(6)} %add.46), channel_id=1, replica_groups=mesh['img'=8,'txt'=4] {'txt'}, use_global_device_ids=true, to_apply=%region_20.0 | all-reduce | flops 1 | bytes 8 | tf_op jit(solution)/shard_map/psum | solution.py:53
  129.1 14.2 %psum.47 = f32[]{:T(128)} all-reduce(f32[]{:T(128)} %psum.46), channel_id=1, replica_groups=mesh['img'=8,'txt'=4] {'img'}, use_global_device_ids=true, to_apply=%region_21.0 | all-reduce | flops 1 | bytes 8 | tf_op jit(solution)/shard_map/psum | solution.py:53
  144.0 1.9 reduce-scatter.3.cloned.1.call-done
  145.9 38.8 %reduce-scatter.5.cloned.1.call-done = f32[128,512]{1,0:T(8,128)} async-done(((f32[1024,512]{1,0:T(8,128)}), f32[128,512]{1,0:T(8,128)}) %reduce-scatter.5.cloned.1.call-update) | async-done | bytes 262160 | tf_op jit(solution)/shard_map/reduce_scatter | solution.py:55
  (2 shorter events, 0.0 us)
Async XLA Ops:
  7.2 1.7 copy-start
  7.2 138.7 %reduce-scatter.3.cloned.1.call-start = ((), (), s32[]{:S(2)}) async-start(), calls=%async_computation.2 | async-start | bytes 2621440 | tf_op jit(solution)/shard_map/reduce_scatter | solution.py:63
  8.9 6.4 %copy-start.2 = (bf16[1024,512]{1,0:T(8,128)(2,1)S(1)}, bf16[1024,512]{1,0:T(8,128)(2,1)}, u32[]{:S(2)}) copy-start(bf16[1024,512]{1,0:T(8,128)(2,1)} %param.7) | copy-start | bytes 3145732
  8.9 6.4 %copy-start.4 = (bf16[1024,512]{1,0:T(8,128)(2,1)S(1)}, bf16[1024,512]{1,0:T(8,128)(2,1)}, u32[]{:S(2)}) copy-start(bf16[1024,512]{1,0:T(8,128)(2,1)} %param.6) | copy-start | bytes 3145732
  104.2 6.4 %copy-start.3 = (bf16[1024,512]{1,0:T(8,128)(2,1)S(1)}, bf16[1024,512]{1,0:T(8,128)(2,1)}, u32[]{:S(2)}) copy-start(bf16[1024,512]{1,0:T(8,128)(2,1)} %param.7) | copy-start | bytes 3145732
  109.2 1.3 copy-start.1
  113.2 71.5 %reduce-scatter.5.cloned.1.call-start = ((), (), s32[]{:S(2)}) async-start(), calls=%async_computation.3 | async-start | bytes 2359296 | tf_op jit(solution)/shard_map/reduce_scatter | solution.py:55
Sparse Core Ops, SparseCore 0:
  113.3 32.5 reduce-scatter.2
  148.7 35.8 reduce-scatter.4
